TPU v7x, 32 devices: a whole 2x2x4 slice. The times are simulated.
32 devices in a mesh: gz: 8 (over z, x), rows: 4 (over y, core).
Axes of the slice: x: 2, y: 2, z: 4, core: 2. Of those that a mesh axis runs over, the one named last changes fastest.
Arguments:
- sections: bfloat16 [8, 1024, 4096], P('gz', 'rows'), may hold values from -4 to 4
- peaks: int32 [8, 2, 1, 4], P('gz'), may hold values from -16 to 16, as said below
Outputs:
- field: float32 [8, 2, 1024, 4096], P('gz', None, 'rows')
- pair_offsets: float32 [8, 2, 1, 4], P('gz')
- residual: bfloat16 [8, 1024, 4096], P('gz', 'rows')
Inputs may be any that keep to these rules, and one draw needn't show every extreme that they name: `peaks`: in every draw the first section's first patch has row offset 16 and column offset -16.
All inputs are finite; a program needn't handle non-finite values.
Results may differ from a plain program's by a relative error of at most 0.001.
Values may be sent and summed in bfloat16 or wider, within the bound.
A program may use at most 64 MiB of HBM per device.

v0:
```python
import functools

import jax
import jax.numpy as jnp
import numpy as np
from jax import lax
from jax.experimental import pallas as pl
from jax.experimental.pallas import tpu as pltpu
from jax.sharding import PartitionSpec as P

PATCH = 1024
MAXOFF = 16
LAMBDA = 0.002
RIDGE = 0.05
EDGE = 32
SIDE = 128
BLOCK = 256
TILE = 64
MESH = pl.DeviceIdType.MESH


def invert_three(matrix):
    a, b, c = (matrix[0, 0], matrix[0, 1], matrix[0, 2])
    d, e, f = (matrix[1, 0], matrix[1, 1], matrix[1, 2])
    g, h, k = (matrix[2, 0], matrix[2, 1], matrix[2, 2])
    cof = np.array(
        [
            [e * k - f * h, c * h - b * k, b * f - c * e],
            [f * g - d * k, a * k - c * g, c * d - a * f],
            [d * h - e * g, b * g - a * h, a * e - b * d],
        ]
    )
    return cof / (a * (e * k - f * h) - b * (d * k - f * g) + c * (d * h - e * g))


def fit_table(pgy, pgx, patch, height, width):
    yy = ((np.arange(pgy) + 0.5) * patch - height / 2.0) / height
    xx = ((np.arange(pgx) + 0.5) * patch - width / 2.0) / width
    design = np.stack([np.repeat(yy, pgx), np.tile(xx, pgy), np.ones(pgy * pgx)], 1)
    ridge_matrix = np.array([[RIDGE, 0.0, 0.0], [0.0, RIDGE, 0.0], [0.0, 0.0, 0.0]])
    gram = design.T @ design + ridge_matrix
    return invert_three(gram) @ design.T


def register(G, R, pgy, pgx, table, peaks_hbm, sec, res_hbm, nodes, prev, cur, res, rmat, cmat, gmat, acc,
             sums, maps, peaks, peak_sem, cur_sem, res_sem, send_sem, recv_sem, rel_send, rel_recv,
             sum_send, sum_recv, map_send, map_recv):
    band, width = sec.shape[1], sec.shape[2]
    height = band * R
    blocks = width // BLOCK
    per_patch = PATCH // BLOCK
    g, r = lax.axis_index("gz"), lax.axis_index("rows")
    f32, bf16 = jnp.float32, jnp.bfloat16

    barrier = pltpu.get_barrier_semaphore()
    for d in range(1, R):
        pl.semaphore_signal(barrier, inc=1, device_id={"rows": lax.rem(r + d, R)}, device_id_type=MESH)
    for d in range(1, G):
        pl.semaphore_signal(barrier, inc=1, device_id={"gz": lax.rem(g + d, G)}, device_id_type=MESH)
    peak_load = pltpu.make_async_copy(peaks_hbm, peaks, peak_sem)
    peak_load.start()
    load = pltpu.make_async_copy(sec.at[0], cur, cur_sem)
    load.start()
    rows_all = band + 2 * EDGE
    prev[:, 0:SIDE] = jnp.zeros((rows_all, SIDE), bf16)
    prev[:, SIDE + width :] = jnp.zeros((rows_all, SIDE), bf16)

    @pl.when(r == 0)
    def _():
        prev[0:EDGE, :] = jnp.zeros((EDGE, width + 2 * SIDE), bf16)

    @pl.when(r == R - 1)
    def _():
        prev[EDGE + band :, :] = jnp.zeros((EDGE, width + 2 * SIDE), bf16)

    pl.semaphore_wait(barrier, R + G - 2)

    ahead = lax.rem(g + 1, G)

    def edge_copy(which):
        row = 0 if which == 0 else band - EDGE
        return pltpu.make_async_remote_copy(
            src_ref=sec.at[0, pl.ds(row, EDGE), :],
            dst_ref=prev.at[pl.ds(EDGE + row, EDGE), pl.ds(SIDE, width)],
            send_sem=send_sem.at[which], recv_sem=recv_sem.at[which],
            device_id={"gz": ahead}, device_id_type=MESH)

    def span_copy(k, col, count):
        return pltpu.make_async_remote_copy(
            src_ref=sec.at[0, pl.ds(EDGE, band - 2 * EDGE), pl.ds(col, count)],
            dst_ref=prev.at[pl.ds(2 * EDGE, band - 2 * EDGE), pl.ds(SIDE + col, count)],
            send_sem=send_sem.at[2 + k], recv_sem=recv_sem.at[2 + k],
            device_id={"gz": ahead}, device_id_type=MESH)

    def head_copy():
        return span_copy(0, 0, BLOCK + SIDE)

    def middle_copy(k):
        return span_copy(k, pl.multiple_of(k * BLOCK + SIDE, SIDE), BLOCK)

    def tail_copy():
        return span_copy(blocks - 1, width - BLOCK + SIDE, BLOCK - SIDE)

    def relay_up():
        return pltpu.make_async_remote_copy(
            src_ref=prev.at[pl.ds(EDGE, EDGE), pl.ds(SIDE, width)],
            dst_ref=prev.at[pl.ds(EDGE + band, EDGE), pl.ds(SIDE, width)],
            send_sem=rel_send.at[0], recv_sem=rel_recv.at[0],
            device_id={"rows": lax.rem(r + R - 1, R)}, device_id_type=MESH)

    def relay_down():
        return pltpu.make_async_remote_copy(
            src_ref=prev.at[pl.ds(band, EDGE), pl.ds(SIDE, width)],
            dst_ref=prev.at[pl.ds(0, EDGE), pl.ds(SIDE, width)],
            send_sem=rel_send.at[1], recv_sem=rel_recv.at[1],
            device_id={"rows": lax.rem(r + 1, R)}, device_id_type=MESH)

    @pl.when(g < G - 1)
    def _():
        edge_copy(0).start()
        edge_copy(1).start()
        head_copy().start()
        lax.fori_loop(1, blocks - 1, lambda k, z: (middle_copy(k).start(), z)[1], 0)
        tail_copy().start()

    @pl.when(g == 0)
    def _():
        def clear(t, z):
            prev[pl.ds(pl.multiple_of(t * EDGE, EDGE), EDGE), :] = jnp.zeros((EDGE, width + 2 * SIDE), bf16)
            return z

        lax.fori_loop(0, rows_all // EDGE, clear, 0)

    patch_row = r * band // PATCH
    peak_load.wait()
    rr = lax.broadcasted_iota(jnp.int32, (TILE, TILE + 2 * EDGE), 0)
    rk = lax.broadcasted_iota(jnp.int32, (TILE, TILE + 2 * EDGE), 1)
    ck = lax.broadcasted_iota(jnp.int32, (BLOCK + 2 * SIDE, BLOCK), 0)
    cn = lax.broadcasted_iota(jnp.int32, (BLOCK + 2 * SIDE, BLOCK), 1)
    rdiff = rk - rr - EDGE
    cdiff = ck - cn - SIDE
    for j in range(pgx):
        a = peaks[0, 0, patch_row, j]
        b = peaks[0, 1, patch_row, j]
        for n, step in enumerate((0, 1, -1)):
            rmat[j, n * TILE : (n + 1) * TILE, :] = jnp.where(rdiff == a + step, 1.0, 0.0).astype(bf16)
        cmat[j] = jnp.where(cdiff == b, 1.0, 0.0).astype(bf16)
        gmat[j] = jnp.where(cdiff == b + 1, 0.5, jnp.where(cdiff == b - 1, -0.5, 0.0)).astype(bf16)
    acc[...] = jnp.zeros_like(acc)
    load.wait()

    @pl.when(g > 0)
    def _():
        edge_copy(0).wait_recv()

        @pl.when(r > 0)
        def _():
            relay_up().start()

        edge_copy(1).wait_recv()

        @pl.when(r < R - 1)
        def _():
            relay_down().start()
            relay_up().wait_recv()

        @pl.when(r > 0)
        def _():
            relay_down().wait_recv()

        head_copy().wait_recv()

    tiles = band // TILE

    def fold(value):
        value = jnp.sum(value.reshape(value.shape[0] // 8, 8, BLOCK), axis=0)
        return sum(value[:, q : q + 128] for q in range(0, BLOCK, 128))

    def out_copy(c):
        col = pl.multiple_of(c * BLOCK, BLOCK)
        return pltpu.make_async_copy(res.at[:, pl.ds(col, BLOCK)], res_hbm.at[0, :, pl.ds(col, BLOCK)], res_sem.at[c])

    def body(c, z):
        @pl.when((g > 0) & (c > 0) & (c < blocks - 1))
        def _():
            middle_copy(c).wait_recv()

        @pl.when((g > 0) & (c == blocks - 1))
        def _():
            tail_copy().wait_recv()

        j = c // per_patch
        col = pl.multiple_of(c * BLOCK, BLOCK)
        moved = []
        for t in range(tiles):
            window = prev[t * TILE : t * TILE + TILE + 2 * EDGE, pl.ds(col, BLOCK + 2 * SIDE)]
            moved.append(jnp.dot(rmat[j], window, preferred_element_type=f32).astype(bf16))
        parts = [jnp.concatenate([m[n * TILE : (n + 1) * TILE] for m in moved], axis=0) for n in range(3)]
        q = jnp.dot(parts[0], cmat[j], preferred_element_type=f32)
        lower = jnp.dot(parts[1], cmat[j], preferred_element_type=f32)
        upper = jnp.dot(parts[2], cmat[j], preferred_element_type=f32)
        gx = jnp.dot(parts[0], gmat[j], preferred_element_type=f32)
        gy = (lower - upper) * 0.5
        e = cur[:, pl.ds(col, BLOCK)].astype(f32) - q
        res[:, pl.ds(col, BLOCK)] = e.astype(bf16)
        out_copy(c).start()
        acc[j, 0] += fold(gy * gy)
        acc[j, 1] += fold(gy * gx)
        acc[j, 2] += fold(gx * gx)
        acc[j, 3] += fold(gy * e)
        acc[j, 4] += fold(gx * e)
        return z

    lax.fori_loop(0, blocks, body, 0)

    lane = lax.broadcasted_iota(jnp.int32, (8, 128), 1)
    row = lax.broadcasted_iota(jnp.int32, (8, 128), 0)
    mine = jnp.zeros((8, 128), f32)
    for j in range(pgx):
        for m in range(5):
            total = jnp.sum(jnp.sum(acc[j, m], axis=0, keepdims=True), axis=1, keepdims=True)
            mine = jnp.where((lane == patch_row * pgx + j) & (row == m), total, mine)
    sums[r] = mine

    def sum_copy(d, slot):
        return pltpu.make_async_remote_copy(
            src_ref=sums.at[slot], dst_ref=sums.at[slot], send_sem=sum_send.at[d], recv_sem=sum_recv.at[d],
            device_id={"rows": lax.rem(r + d, R)}, device_id_type=MESH)

    for d in range(1, R):
        sum_copy(d, r).start()
    peak_y = jnp.zeros((1, 128), f32)
    peak_x = jnp.zeros((1, 128), f32)
    for i in range(pgy):
        for j in range(pgx):
            here = lane[0:1] == i * pgx + j
            peak_y = jnp.where(here, peaks[0, 0, i, j].astype(f32), peak_y)
            peak_x = jnp.where(here, peaks[0, 1, i, j].astype(f32), peak_x)
    for d in range(1, R):
        sum_copy(d, lax.rem(r + R - d, R)).wait_recv()
    full = sums[0]
    for k in range(1, R):
        full = full + sums[k]

    damping = LAMBDA * PATCH * PATCH
    first = full[0:1] + damping
    cross = full[1:2]
    second = full[2:3] + damping
    det = first * second - cross * cross
    off_y = peak_y + (second * full[3:4] - cross * full[4:5]) / det
    off_x = peak_x + (first * full[4:5] - cross * full[3:4]) / det
    ty = jnp.zeros((1, 128), f32)
    tx = jnp.zeros((1, 128), f32)
    for p in range(pgy * pgx):
        ty = jnp.where(lane[0:1] == p, float(table[0, p]), ty)
        tx = jnp.where(lane[0:1] == p, float(table[1, p]), tx)

    def lanes(value):
        return jnp.sum(value, axis=1, keepdims=True)

    pieces = [
        off_y,
        off_x,
        1.0 + lanes(off_y * ty) / height,
        lanes(off_y * tx) / width,
        lanes(off_x * ty) / height,
        1.0 + lanes(off_x * tx) / width,
    ]
    own = jnp.zeros((8, 128), f32)
    for k, piece in enumerate(pieces):
        own = jnp.where(row == k, jnp.broadcast_to(piece, (8, 128)), own)
    maps[g] = own

    def map_copy(d, slot):
        return pltpu.make_async_remote_copy(
            src_ref=maps.at[slot], dst_ref=maps.at[slot], send_sem=map_send.at[d], recv_sem=map_recv.at[d],
            device_id={"gz": lax.rem(g + d, G)}, device_id_type=MESH)

    for d in reversed(range(1, G)):
        @pl.when(g + d < G)
        def _():
            map_copy(d, g).start()

    lax.fori_loop(0, blocks, lambda c, z: (out_copy(c).wait(), z)[1], 0)

    @pl.when(g < G - 1)
    def _():
        edge_copy(0).wait_send()
        edge_copy(1).wait_send()
        head_copy().wait_send()
        lax.fori_loop(1, blocks - 1, lambda k, z: (middle_copy(k).wait_send(), z)[1], 0)
        tail_copy().wait_send()

    @pl.when((g > 0) & (r > 0))
    def _():
        relay_up().wait_send()

    @pl.when((g > 0) & (r < R - 1))
    def _():
        relay_down().wait_send()

    for d in range(1, R):
        sum_copy(d, r).wait_send()
    for d in range(1, G):
        @pl.when(g - d >= 0)
        def _():
            map_copy(d, lax.rem(g + G - d, G)).wait_recv()

    def advance(s, u):
        uy, ux = u
        m = maps[s]
        return (m[2:3] * uy + m[3:4] * ux + m[0:1], m[4:5] * uy + m[5:6] * ux + m[1:2])

    zero = jnp.zeros((1, 128), f32)
    uy, ux = lax.fori_loop(0, g + 1, advance, (zero, zero))
    nodes[0:1] = uy
    nodes[1:2] = ux
    nodes[2:3] = off_y
    nodes[3:4] = off_x
    nodes[4:8] = jnp.zeros((4, 128), f32)

    for d in range(1, G):
        @pl.when(g + d < G)
        def _():
            map_copy(d, g).wait_send()


def spread_out(pgy, pgx, start_ref, nodes, res_in, field, offsets, res_out, buf, stage, in_sem, out_sem, field_sem):
    band, width = field.shape[2], field.shape[3]
    f32 = jnp.float32
    fetch = pltpu.make_async_copy(res_in, stage, in_sem)
    fetch.start()
    cols = (lax.broadcasted_iota(jnp.int32, (8, width), 1).astype(f32) + 0.5) / PATCH - 0.5
    cols = jnp.clip(cols, 0.0, pgx - 1.0)
    weights = [jnp.maximum(0.0, 1.0 - jnp.abs(cols - j)) for j in range(pgx)]
    part = 32
    put = pltpu.make_async_copy(stage, res_out, out_sem)
    copies = []
    for k in range(2):
        wide = []
        for i in range(pgy):
            line = jnp.zeros((8, width), f32)
            for j in range(pgx):
                p = i * pgx + j
                line = line + weights[j] * nodes[k : k + 1, p : p + 1]
            wide.append(line)
        for t in range(band // part):
            slot = 0 if pgy == 1 else t
            for q in range(0, part, 8) if pgy > 1 or t == 0 else ():
                if pgy == 1:
                    block = wide[0]
                else:
                    rows = lax.broadcasted_iota(jnp.int32, (8, 1), 0).astype(f32) + start_ref[0].astype(f32)
                    pos = jnp.clip((rows + (t * part + q + 0.5)) / PATCH - 0.5, 0.0, pgy - 1.0)
                    block = sum(jnp.maximum(0.0, 1.0 - jnp.abs(pos - i)) * wide[i] for i in range(pgy))
                buf[k, slot * part + q : slot * part + q + 8, :] = block
            copy = pltpu.make_async_copy(
                buf.at[k, pl.ds(slot * part, part), :], field.at[0, k, pl.ds(t * part, part), :],
                field_sem.at[len(copies)])
            copy.start()
            copies.append(copy)
        if k == 0:
            fetch.wait()
            put.start()
    offsets[...] = nodes[2:4, 0 : pgy * pgx]
    put.wait()
    for copy in copies:
        copy.wait()


def per_device(G, R, sections, peaks):
    band, width = sections.shape[1:]
    height = band * R
    pgy, pgx = height // PATCH, width // PATCH
    blocks = width // BLOCK
    f32, bf16 = jnp.float32, jnp.bfloat16
    table = fit_table(pgy, pgx, PATCH, height, width).astype(np.float32)
    vmem = pl.BlockSpec(memory_space=pltpu.VMEM)
    smem = pl.BlockSpec(memory_space=pltpu.SMEM)
    anywhere = pl.BlockSpec(memory_space=pl.ANY)
    dma = pltpu.SemaphoreType.DMA
    residual, nodes = pl.pallas_call(
        functools.partial(register, G, R, pgy, pgx, table),
        name="register",
        out_shape=(jax.ShapeDtypeStruct((1, band, width), bf16), jax.ShapeDtypeStruct((8, 128), f32)),
        in_specs=[anywhere, anywhere],
        out_specs=(anywhere, vmem),
        scratch_shapes=[
            pltpu.VMEM((band + 2 * EDGE, width + 2 * SIDE), bf16),
            pltpu.VMEM((band, width), bf16),
            pltpu.VMEM((band, width), bf16),
            pltpu.VMEM((pgx, 3 * TILE, TILE + 2 * EDGE), bf16),
            pltpu.VMEM((pgx, BLOCK + 2 * SIDE, BLOCK), bf16),
            pltpu.VMEM((pgx, BLOCK + 2 * SIDE, BLOCK), bf16),
            pltpu.VMEM((pgx, 5, 8, 128), f32),
            pltpu.VMEM((R, 8, 128), f32),
            pltpu.VMEM((G, 8, 128), f32),
            pltpu.SMEM((1, 2, pgy, pgx), jnp.int32),
            dma, dma, dma((blocks,)), dma((blocks + 2,)), dma((blocks + 2,)), dma((2,)), dma((2,)),
            dma((R,)), dma((R,)), dma((G,)), dma((G,)),
        ],
        compiler_params=pltpu.CompilerParams(collective_id=0, has_side_effects=True),
    )(peaks, sections)
    start = (lax.axis_index("rows") * band).astype(jnp.int32).reshape(1)
    field, offsets, residual = pl.pallas_call(
        functools.partial(spread_out, pgy, pgx),
        name="spread_out",
        out_shape=(
            jax.ShapeDtypeStruct((1, 2, band, width), f32),
            jax.ShapeDtypeStruct((2, pgy * pgx), f32),
            jax.ShapeDtypeStruct((1, band, width), bf16),
        ),
        in_specs=[smem, vmem, anywhere],
        out_specs=(anywhere, vmem, anywhere),
        scratch_shapes=[
            pltpu.VMEM((2, 32 if pgy == 1 else band, width), f32), pltpu.VMEM((1, band, width), bf16),
            dma, dma, dma((2 * (band // 32),)),
        ],
    )(start, nodes, residual)
    return field, offsets.reshape(1, 2, pgy, pgx), residual


def solution(mesh):
    return jax.shard_map(
        functools.partial(per_device, mesh.shape["gz"], mesh.shape["rows"]),
        mesh=mesh,
        in_specs=(P("gz", "rows", None), P("gz", None, None, None)),
        out_specs=(P("gz", None, "rows", None), P("gz", None, None, None), P("gz", "rows", None)),
        check_vma=False,
    )
```

profile of v0, /device:TPU:8, one launch (start us, length us, event | category | flops | bytes accessed | tf_op | source)
XLA Modules:
  0.0 66.8 jit_solution(1073576123501033459)
XLA Ops:
  0.6 59.5 %register.1 = (bf16[1,256,4096]{2,1,0:T(8,128)(2,1)}, f32[8,128]{1,0:T(8,128)}) custom-call(s32[1,2,1,4]{3,2,1,0:T(1,128)} %peaks_hbm.1, bf16[1,256,4096]{2,1,0:T(8,128)(2,1)} %sec.1), custom_call_target="tpu_custom_call" | custom-call | tf_op jit(solution)/shard_map/register/pallas_call | solution.py:382
  60.1 6.7 %spread_out.1 = (f32[1,2,256,4096]{3,2,1,0:T(8,128)}, f32[2,4]{1,0:T(2,128)}, bf16[1,256,4096]{2,1,0:T(8,128)(2,1)}) custom-call(s32[1]{0:T(128)} %bitcast.start_ref, f32[8,128]{1,0:T(8,128)} %get-tuple-element.8.nodes, bf16[1,256,4096]{2,1,0:T(8,128)(2,1)} %get-tuple-element.9.res_in), custom_call_target="tpu_custom_call" | custom-call | tf_op jit(solution)/shard_map/spread_out/pallas_call | solution.py:405
where the time goes:
time: 67 us; the launch traced here: 66.8 us
  Pallas kernels  66.2 us (99%)
    pallas_call x1, Pallas kernels, per_device(): pl.pallas_call(functools.partial(register, G, R, pgy, pgx, table), name='...  59.5 us
    pallas_call x1, Pallas kernels, per_device(): pl.pallas_call(functools.partial(spread_out, pgy, pgx), name='spread_out'...  6.71 us

commit v1 on v0

v1 whole, which is shorter than its diff:
```python
import functools

import jax
import jax.numpy as jnp
import numpy as np
from jax import lax
from jax.experimental import pallas as pl
from jax.experimental.pallas import tpu as pltpu
from jax.sharding import PartitionSpec as P

PATCH = 1024
MAXOFF = 16
LAMBDA = 0.002
RIDGE = 0.05
EDGE = 32
SIDE = 128
BLOCK = 256
TILE = 64
MESH = pl.DeviceIdType.MESH


def invert_three(matrix):
    a, b, c = (matrix[0, 0], matrix[0, 1], matrix[0, 2])
    d, e, f = (matrix[1, 0], matrix[1, 1], matrix[1, 2])
    g, h, k = (matrix[2, 0], matrix[2, 1], matrix[2, 2])
    cof = np.array(
        [
            [e * k - f * h, c * h - b * k, b * f - c * e],
            [f * g - d * k, a * k - c * g, c * d - a * f],
            [d * h - e * g, b * g - a * h, a * e - b * d],
        ]
    )
    return cof / (a * (e * k - f * h) - b * (d * k - f * g) + c * (d * h - e * g))


def fit_table(pgy, pgx, patch, height, width):
    yy = ((np.arange(pgy) + 0.5) * patch - height / 2.0) / height
    xx = ((np.arange(pgx) + 0.5) * patch - width / 2.0) / width
    design = np.stack([np.repeat(yy, pgx), np.tile(xx, pgy), np.ones(pgy * pgx)], 1)
    ridge_matrix = np.array([[RIDGE, 0.0, 0.0], [0.0, RIDGE, 0.0], [0.0, 0.0, 0.0]])
    gram = design.T @ design + ridge_matrix
    return invert_three(gram) @ design.T


def register(G, R, pgy, pgx, table, peaks_hbm, sec, res, nodes, prev, cur, rmat, cmat, gmat, acc,
             gather, extra, peaks, peak_sem, cur_sem, ready, send_sem, recv_sem, rel_send, rel_recv,
             sum_send, sum_recv):
    band, width = sec.shape[1], sec.shape[2]
    height = band * R
    blocks = width // BLOCK
    per_patch = PATCH // BLOCK
    patches = pgy * pgx
    g, r = lax.axis_index("gz"), lax.axis_index("rows")
    f32, bf16 = jnp.float32, jnp.bfloat16

    spans = ((0, EDGE), (band - EDGE, EDGE), (EDGE, band - 2 * EDGE))

    def load(k):
        rows = pl.ds(*spans[k])
        return pltpu.make_async_copy(sec.at[0, rows, :], cur.at[rows, :], cur_sem.at[k])

    gather[...] = jnp.zeros_like(gather)
    barrier = pltpu.get_barrier_semaphore()

    @pl.when(g > 0)
    def _():
        pl.semaphore_signal(barrier, inc=1, device_id={"gz": g - 1}, device_id_type=MESH)

    for k in range(3):
        load(k).start()
    peak_load = pltpu.make_async_copy(peaks_hbm, peaks, peak_sem)
    peak_load.start()
    for d in range(1, R):
        pl.semaphore_signal(barrier, inc=1, device_id={"rows": lax.rem(r + d, R)}, device_id_type=MESH)

    @pl.when(g < G - 1)
    def _():
        pl.semaphore_signal(barrier, inc=1, device_id={"gz": g + 1}, device_id_type=MESH)

    pl.semaphore_wait(barrier, R - 1 + jnp.where(g > 0, 1, 0) + jnp.where(g < G - 1, 1, 0))
    rows_all = band + 2 * EDGE
    ahead = lax.rem(g + 1, G)

    def edge_copy(which):
        row = 0 if which == 0 else band - EDGE
        return pltpu.make_async_remote_copy(
            src_ref=cur.at[pl.ds(row, EDGE), :],
            dst_ref=prev.at[pl.ds(EDGE + row, EDGE), pl.ds(SIDE, width)],
            send_sem=send_sem.at[which], recv_sem=recv_sem.at[which],
            device_id={"gz": ahead}, device_id_type=MESH)

    def span_copy(k, col, count):
        return pltpu.make_async_remote_copy(
            src_ref=cur.at[pl.ds(EDGE, band - 2 * EDGE), pl.ds(col, count)],
            dst_ref=prev.at[pl.ds(2 * EDGE, band - 2 * EDGE), pl.ds(SIDE + col, count)],
            send_sem=send_sem.at[2 + k], recv_sem=recv_sem.at[2 + k],
            device_id={"gz": ahead}, device_id_type=MESH)

    def head_copy():
        return span_copy(0, 0, BLOCK + SIDE)

    def middle_copy(k):
        return span_copy(k, pl.multiple_of(k * BLOCK + SIDE, SIDE), BLOCK)

    def tail_copy():
        return span_copy(blocks - 1, width - BLOCK + SIDE, BLOCK - SIDE)

    def relay_up():
        return pltpu.make_async_remote_copy(
            src_ref=prev.at[pl.ds(EDGE, EDGE), pl.ds(SIDE, width)],
            dst_ref=prev.at[pl.ds(EDGE + band, EDGE), pl.ds(SIDE, width)],
            send_sem=rel_send.at[0], recv_sem=rel_recv.at[0],
            device_id={"rows": lax.rem(r + R - 1, R)}, device_id_type=MESH)

    def relay_down():
        return pltpu.make_async_remote_copy(
            src_ref=prev.at[pl.ds(band, EDGE), pl.ds(SIDE, width)],
            dst_ref=prev.at[pl.ds(0, EDGE), pl.ds(SIDE, width)],
            send_sem=rel_send.at[1], recv_sem=rel_recv.at[1],
            device_id={"rows": lax.rem(r + 1, R)}, device_id_type=MESH)

    for which in (0, 1):
        load(which).wait()

        @pl.when(g < G - 1)
        def _():
            edge_copy(which).start()

    load(2).wait()

    @pl.when(g < G - 1)
    def _():
        head_copy().start()
        lax.fori_loop(1, blocks - 1, lambda k, z: (middle_copy(k).start(), z)[1], 0)
        tail_copy().start()

    prev[:, 0:SIDE] = jnp.zeros((rows_all, SIDE), bf16)
    prev[:, SIDE + width :] = jnp.zeros((rows_all, SIDE), bf16)

    @pl.when(r == 0)
    def _():
        prev[0:EDGE, :] = jnp.zeros((EDGE, width + 2 * SIDE), bf16)

    @pl.when(r == R - 1)
    def _():
        prev[EDGE + band :, :] = jnp.zeros((EDGE, width + 2 * SIDE), bf16)

    @pl.when(g == 0)
    def _():
        def clear(t, z):
            prev[pl.ds(pl.multiple_of(t * EDGE, EDGE), EDGE), :] = jnp.zeros((EDGE, width + 2 * SIDE), bf16)
            return z

        lax.fori_loop(0, rows_all // EDGE, clear, 0)

    patch_row = r * band // PATCH
    peak_load.wait()
    rr = lax.broadcasted_iota(jnp.int32, (TILE, TILE + 2 * EDGE), 0)
    rk = lax.broadcasted_iota(jnp.int32, (TILE, TILE + 2 * EDGE), 1)
    ck = lax.broadcasted_iota(jnp.int32, (BLOCK + 2 * SIDE, BLOCK), 0)
    cn = lax.broadcasted_iota(jnp.int32, (BLOCK + 2 * SIDE, BLOCK), 1)
    rdiff = rk - rr - EDGE
    cdiff = ck - cn - SIDE
    for j in range(pgx):
        a = peaks[0, 0, patch_row, j]
        b = peaks[0, 1, patch_row, j]
        for n, step in enumerate((0, 1, -1)):
            rmat[j, n * TILE : (n + 1) * TILE, :] = jnp.where(rdiff == a + step, 1.0, 0.0).astype(bf16)
        cmat[j] = jnp.where(cdiff == b, 1.0, 0.0).astype(bf16)
        gmat[j] = jnp.where(cdiff == b + 1, 0.5, jnp.where(cdiff == b - 1, -0.5, 0.0)).astype(bf16)
    acc[...] = jnp.zeros_like(acc)

    lane = lax.broadcasted_iota(jnp.int32, (1, 128), 1)
    own_peaks = jnp.zeros((1, 128), f32)
    for i in range(pgy):
        for j in range(pgx):
            p = i * pgx + j
            own_peaks = jnp.where(lane == 5 * patches + p, peaks[0, 0, i, j].astype(f32), own_peaks)
            own_peaks = jnp.where(lane == 6 * patches + p, peaks[0, 1, i, j].astype(f32), own_peaks)
    extra[...] = jnp.where(r == 0, own_peaks, jnp.zeros((1, 128), f32))

    @pl.when(g < G - 1)
    def _():
        pl.semaphore_wait(ready, 1)

    @pl.when(g > 0)
    def _():
        pl.semaphore_signal(ready, inc=1, device_id={"gz": g - 1}, device_id_type=MESH)
        edge_copy(0).wait_recv()

        @pl.when(r > 0)
        def _():
            relay_up().start()

        edge_copy(1).wait_recv()

        @pl.when(r < R - 1)
        def _():
            relay_down().start()
            relay_up().wait_recv()

        @pl.when(r > 0)
        def _():
            relay_down().wait_recv()

        head_copy().wait_recv()

    tiles = band // TILE

    def fold(value):
        value = jnp.sum(value.reshape(value.shape[0] // 8, 8, BLOCK), axis=0)
        return sum(value[:, q : q + 128] for q in range(0, BLOCK, 128))

    def body(c, z):
        @pl.when((g > 0) & (c > 0) & (c < blocks - 1))
        def _():
            middle_copy(c).wait_recv()

        @pl.when((g > 0) & (c == blocks - 1))
        def _():
            tail_copy().wait_recv()

        j = c // per_patch
        col = pl.multiple_of(c * BLOCK, BLOCK)
        moved = []
        for t in range(tiles):
            window = prev[t * TILE : t * TILE + TILE + 2 * EDGE, pl.ds(col, BLOCK + 2 * SIDE)]
            moved.append(jnp.dot(rmat[j], window, preferred_element_type=f32).astype(bf16))
        parts = [jnp.concatenate([m[n * TILE : (n + 1) * TILE] for m in moved], axis=0) for n in range(3)]
        q = jnp.dot(parts[0], cmat[j], preferred_element_type=f32)
        lower = jnp.dot(parts[1], cmat[j], preferred_element_type=f32)
        upper = jnp.dot(parts[2], cmat[j], preferred_element_type=f32)
        gx = jnp.dot(parts[0], gmat[j], preferred_element_type=f32)
        gy = (lower - upper) * 0.5
        e = cur[:, pl.ds(col, BLOCK)].astype(f32) - q
        res[0, :, pl.ds(col, BLOCK)] = e.astype(bf16)
        for m, value in enumerate((gy * gy, gy * gx, gx * gx, gy * e, gx * e)):
            at = pl.ds(pl.multiple_of((m * pgx + j) * 8, 8), 8)
            acc[at, :] = acc[at, :] + fold(value)
        return z

    lax.fori_loop(0, blocks, body, 0)

    count = acc.shape[0] // 8
    totals = acc[pl.ds(0, count, stride=8), :]
    for k in range(1, 8):
        totals = totals + acc[pl.ds(k, count, stride=8), :]
    totals = jnp.sum(totals, axis=1, keepdims=True)
    place = lax.broadcasted_iota(jnp.int32, (count, 128), 0)
    for m in range(1, 5):
        place = place + jnp.where(lax.broadcasted_iota(jnp.int32, (count, 128), 0) >= m * pgx, patches - pgx, 0)
    hit = lax.broadcasted_iota(jnp.int32, (count, 128), 1) == place + patch_row * pgx
    mine = jnp.sum(jnp.where(hit, totals, 0.0), axis=0, keepdims=True)
    gather[r, pl.ds(g, 1), :] = mine + extra[...]

    def sum_copy(d, k):
        return pltpu.make_async_remote_copy(
            src_ref=gather.at[r, pl.ds(g, 1), :], dst_ref=gather.at[r, pl.ds(g, 1), :],
            send_sem=sum_send.at[d * R + k], recv_sem=sum_recv.at[r * G + g],
            device_id={"gz": g + d, "rows": lax.rem(r + k, R)}, device_id_type=MESH)

    def sum_arrival(s, k):
        origin = lax.rem(r + k, R)
        return pltpu.make_async_remote_copy(
            src_ref=gather.at[origin, pl.ds(s, 1), :], dst_ref=gather.at[origin, pl.ds(s, 1), :],
            send_sem=sum_send.at[0], recv_sem=sum_recv.at[origin * G + s],
            device_id={"rows": lax.rem(r + 1, R)}, device_id_type=MESH)

    def send_sums(i, z):
        d = G - 1 - g - i
        for k in range(R):
            if k:
                sum_copy(d, k).start()
            else:
                @pl.when(d > 0)
                def _():
                    sum_copy(d, k).start()
        return z

    lax.fori_loop(0, G - g, send_sums, 0)

    @pl.when(g < G - 1)
    def _():
        edge_copy(0).wait_send()
        edge_copy(1).wait_send()
        head_copy().wait_send()
        lax.fori_loop(1, blocks - 1, lambda k, z: (middle_copy(k).wait_send(), z)[1], 0)
        tail_copy().wait_send()

    @pl.when((g > 0) & (r > 0))
    def _():
        relay_up().wait_send()

    @pl.when((g > 0) & (r < R - 1))
    def _():
        relay_down().wait_send()

    def settle_sums(d, z):
        for k in range(R):
            if k:
                sum_copy(d, k).wait_send()
            else:
                @pl.when(d > 0)
                def _():
                    sum_copy(d, k).wait_send()
        return z

    lax.fori_loop(0, G - g, settle_sums, 0)

    def await_sums(s, z):
        for k in range(R):
            if k:
                sum_arrival(s, k).wait_recv()
            else:
                @pl.when(s < g)
                def _():
                    sum_arrival(s, k).wait_recv()
        return z

    lax.fori_loop(0, g + 1, await_sums, 0)

    full = gather[0]
    for k in range(1, R):
        full = full + gather[k]

    def moment(m):
        return pltpu.roll(full, 128 - m * patches, 1)

    damping = LAMBDA * PATCH * PATCH
    first = full + damping
    cross = moment(1)
    second = moment(2) + damping
    pull_y = moment(3)
    pull_x = moment(4)
    det = first * second - cross * cross
    valid = lax.broadcasted_iota(jnp.int32, (G, 128), 1) < patches
    off_y = jnp.where(valid, moment(5) + (second * pull_y - cross * pull_x) / det, 0.0)
    off_x = jnp.where(valid, moment(6) + (first * pull_x - cross * pull_y) / det, 0.0)
    ty = jnp.zeros((1, 128), f32)
    tx = jnp.zeros((1, 128), f32)
    for p in range(patches):
        ty = jnp.where(lane == p, float(table[0, p]), ty)
        tx = jnp.where(lane == p, float(table[1, p]), tx)

    def lanes(value):
        return jnp.broadcast_to(jnp.sum(value, axis=1, keepdims=True), (G, 128))

    yy = 1.0 + lanes(off_y * ty) / height
    yx = lanes(off_y * tx) / width
    xy = lanes(off_x * ty) / height
    xx = 1.0 + lanes(off_x * tx) / width
    uy = jnp.zeros((1, 128), f32)
    ux = jnp.zeros((1, 128), f32)
    for s in range(G):
        at = slice(s, s + 1)
        step_y = yy[at] * uy + yx[at] * ux + off_y[at]
        step_x = xy[at] * uy + xx[at] * ux + off_x[at]
        uy = jnp.where(s <= g, step_y, uy)
        ux = jnp.where(s <= g, step_x, ux)
    chosen = lax.broadcasted_iota(jnp.int32, (G, 128), 0) == g
    nodes[0:1] = uy
    nodes[1:2] = ux
    nodes[2:3] = jnp.sum(jnp.where(chosen, off_y, 0.0), axis=0, keepdims=True)
    nodes[3:4] = jnp.sum(jnp.where(chosen, off_x, 0.0), axis=0, keepdims=True)
    nodes[4:8] = jnp.zeros((4, 128), f32)


def spread_out(pgy, pgx, start_ref, nodes, res_in, field, offsets, res_out, buf, out_sem, field_sem):
    band, width = field.shape[2], field.shape[3]
    f32 = jnp.float32
    put = pltpu.make_async_copy(res_in, res_out, out_sem)
    put.start()
    cols = (lax.broadcasted_iota(jnp.int32, (8, width), 1).astype(f32) + 0.5) / PATCH - 0.5
    cols = jnp.clip(cols, 0.0, pgx - 1.0)
    weights = [jnp.maximum(0.0, 1.0 - jnp.abs(cols - j)) for j in range(pgx)]
    part = 32
    copies = []
    for k in range(2):
        wide = []
        for i in range(pgy):
            line = jnp.zeros((8, width), f32)
            for j in range(pgx):
                p = i * pgx + j
                line = line + weights[j] * nodes[k : k + 1, p : p + 1]
            wide.append(line)
        for t in range(band // part):
            slot = 0 if pgy == 1 else t
            for q in range(0, part, 8) if pgy > 1 or t == 0 else ():
                if pgy == 1:
                    block = wide[0]
                else:
                    rows = lax.broadcasted_iota(jnp.int32, (8, 1), 0).astype(f32) + start_ref[0].astype(f32)
                    pos = jnp.clip((rows + (t * part + q + 0.5)) / PATCH - 0.5, 0.0, pgy - 1.0)
                    block = sum(jnp.maximum(0.0, 1.0 - jnp.abs(pos - i)) * wide[i] for i in range(pgy))
                buf[k, slot * part + q : slot * part + q + 8, :] = block
            copy = pltpu.make_async_copy(
                buf.at[k, pl.ds(slot * part, part), :], field.at[0, k, pl.ds(t * part, part), :],
                field_sem.at[len(copies)])
            copy.start()
            copies.append(copy)
    offsets[...] = nodes[2:4, 0 : pgy * pgx]
    put.wait()
    for copy in copies:
        copy.wait()


def per_device(G, R, sections, peaks):
    band, width = sections.shape[1:]
    height = band * R
    pgy, pgx = height // PATCH, width // PATCH
    blocks = width // BLOCK
    f32, bf16 = jnp.float32, jnp.bfloat16
    table = fit_table(pgy, pgx, PATCH, height, width).astype(np.float32)
    vmem = pl.BlockSpec(memory_space=pltpu.VMEM)
    smem = pl.BlockSpec(memory_space=pltpu.SMEM)
    anywhere = pl.BlockSpec(memory_space=pl.ANY)
    dma = pltpu.SemaphoreType.DMA
    padded = -(-5 * pgx // 8) * 8
    residual, nodes = pl.pallas_call(
        functools.partial(register, G, R, pgy, pgx, table),
        name="register",
        out_shape=(jax.ShapeDtypeStruct((1, band, width), bf16), jax.ShapeDtypeStruct((8, 128), f32)),
        in_specs=[anywhere, anywhere],
        out_specs=(vmem, vmem),
        scratch_shapes=[
            pltpu.VMEM((band + 2 * EDGE, width + 2 * SIDE), bf16),
            pltpu.VMEM((band, width), bf16),
            pltpu.VMEM((pgx, 3 * TILE, TILE + 2 * EDGE), bf16),
            pltpu.VMEM((pgx, BLOCK + 2 * SIDE, BLOCK), bf16),
            pltpu.VMEM((pgx, BLOCK + 2 * SIDE, BLOCK), bf16),
            pltpu.VMEM((8 * padded, 128), f32),
            pltpu.VMEM((R, G, 128), f32),
            pltpu.VMEM((1, 128), f32),
            pltpu.SMEM((1, 2, pgy, pgx), jnp.int32),
            dma, dma((3,)), pltpu.SemaphoreType.REGULAR, dma((blocks + 2,)), dma((blocks + 2,)), dma((2,)), dma((2,)),
            dma((G * R,)), dma((G * R,)),
        ],
        compiler_params=pltpu.CompilerParams(collective_id=0, has_side_effects=True, vmem_limit_bytes=20 * 2**20),
    )(peaks, sections)
    start = (lax.axis_index("rows") * band).astype(jnp.int32).reshape(1)
    field, offsets, residual = pl.pallas_call(
        functools.partial(spread_out, pgy, pgx),
        name="spread_out",
        out_shape=(
            jax.ShapeDtypeStruct((1, 2, band, width), f32),
            jax.ShapeDtypeStruct((2, pgy * pgx), f32),
            jax.ShapeDtypeStruct((1, band, width), bf16),
        ),
        in_specs=[smem, vmem, vmem],
        out_specs=(anywhere, vmem, anywhere),
        scratch_shapes=[pltpu.VMEM((2, 32 if pgy == 1 else band, width), f32), dma, dma((2 * (band // 32),))],
        compiler_params=pltpu.CompilerParams(vmem_limit_bytes=20 * 2**20),
    )(start, nodes, residual)
    return field, offsets.reshape(1, 2, pgy, pgx), residual


def solution(mesh):
    return jax.shard_map(
        functools.partial(per_device, mesh.shape["gz"], mesh.shape["rows"]),
        mesh=mesh,
        in_specs=(P("gz", "rows", None), P("gz", None, None, None)),
        out_specs=(P("gz", None, "rows", None), P("gz", None, None, None), P("gz", "rows", None)),
        check_vma=False,
    )
```

time: 67 us -> 61.4 us (0.916)
  Pallas kernels: 66.2 us -> 58.3 us
  local copies, waits for them, and re-layouts: 0 us -> 2.26 us
    pallas_call x1, Pallas kernels: 59.5 us -> 53.7 us  [per_device(): pl.pallas_call(functools.partial(register, G, R, pgy, pgx, table), name='...]
    unnamed x0 -> x4, local copies, waits for them, and re-layouts: none -> 2.26 us
    pallas_call x1, Pallas kernels: 6.71 us -> 4.62 us  [per_device(): pl.pallas_call(functools.partial(spread_out, pgy, pgx), name='spread_out'...]
where the time goes in v1:
time: 61.4 us; the launch traced here: 61.2 us
  Pallas kernels  58.3 us (95%)
  local copies, waits for them, and re-layouts  2.26 us (4%)
  between operations  0.65 us (1%)
    pallas_call x1, Pallas kernels, per_device(): pl.pallas_call(functools.partial(register, G, R, pgy, pgx, table), name='...  53.7 us
    pallas_call x1, Pallas kernels, per_device(): pl.pallas_call(functools.partial(spread_out, pgy, pgx), name='spread_out'...  4.62 us
    unnamed x4, local copies, waits for them, and re-layouts  2.26 us

profile of v1, /device:TPU:8, one launch (start us, length us, event | category | flops | bytes accessed | tf_op | source)
XLA Modules:
  0.0 61.2 jit_solution(12644185118555445952)
XLA Ops:
  0.6 0.0 copy-start
  0.6 1.6 %copy-done = bf16[1,256,4096]{2,1,0:T(8,128)(2,1)S(1)} copy-done((bf16[1,256,4096]{2,1,0:T(8,128)(2,1)S(1)}, bf16[1,256,4096]{2,1,0:T(8,128)(2,1)}, u32[]{:S(2)}) %copy-start) | copy-done | bytes 2097176
  2.2 0.0 copy-start.1
  2.2 0.7 %copy-done.1 = s32[1,2,1,4]{3,2,1,0:T(1,128)S(1)} copy-done((s32[1,2,1,4]{3,2,1,0:T(1,128)S(1)}, s32[1,2,1,4]{3,2,1,0:T(1,128)}, u32[]{:S(2)}) %copy-start.1) | copy-done | bytes 56
  2.9 53.7 %register.1 = (bf16[1,256,4096]{2,1,0:T(8,128)(2,1)S(1)}, f32[8,128]{1,0:T(8,128)S(1)}) custom-call(s32[1,2,1,4]{3,2,1,0:T(1,128)S(1)} %copy-done.1, bf16[1,256,4096]{2,1,0:T(8,128)(2,1)S(1)} %copy-done), custom_call_target="tpu_custom_call" | custom-call | tf_op jit(solution)/shard_map/register/pallas_call | solution.py:419
  56.6 4.6 %spread_out.1 = (f32[1,2,256,4096]{3,2,1,0:T(8,128)}, f32[2,4]{1,0:T(2,128)}, bf16[1,256,4096]{2,1,0:T(8,128)(2,1)}) custom-call(s32[1]{0:T(128)} %bitcast.start_ref, f32[8,128]{1,0:T(8,128)S(1)} %get-tuple-element.8.nodes, bf16[1,256,4096]{2,1,0:T(8,128)(2,1)S(1)} %get-tuple-element.9.res_in), custom_call_target="tpu_custom_call" | custom-call | tf_op jit(solution)/shard_map/spread_out/pallas_call | solution.py:441
Async XLA Ops:
  0.6 1.6 %copy-start = (bf16[1,256,4096]{2,1,0:T(8,128)(2,1)S(1)}, bf16[1,256,4096]{2,1,0:T(8,128)(2,1)}, u32[]{:S(2)}) copy-start(bf16[1,256,4096]{2,1,0:T(8,128)(2,1)} %sec.1) | copy-start | bytes 6291460
  2.2 0.7 %copy-start.1 = (s32[1,2,1,4]{3,2,1,0:T(1,128)S(1)}, s32[1,2,1,4]{3,2,1,0:T(1,128)}, u32[]{:S(2)}) copy-start(s32[1,2,1,4]{3,2,1,0:T(1,128)} %peaks_hbm.1) | copy-start | bytes 100

commit v2 on v1

--- a/solution.py
+++ b/solution.py
@@ -16,6 +16,7 @@
 SIDE = 128
 BLOCK = 256
 TILE = 64
+GROUP = 4
 MESH = pl.DeviceIdType.MESH
 
 
@@ -70,14 +71,17 @@
         load(k).start()
     peak_load = pltpu.make_async_copy(peaks_hbm, peaks, peak_sem)
     peak_load.start()
-    for d in range(1, R):
-        pl.semaphore_signal(barrier, inc=1, device_id={"rows": lax.rem(r + d, R)}, device_id_type=MESH)
+
+    @pl.when(r < R - 1)
+    def _():
+        pl.semaphore_signal(barrier, inc=1, device_id={"rows": r + 1}, device_id_type=MESH)
 
     @pl.when(g < G - 1)
     def _():
         pl.semaphore_signal(barrier, inc=1, device_id={"gz": g + 1}, device_id_type=MESH)
 
-    pl.semaphore_wait(barrier, R - 1 + jnp.where(g > 0, 1, 0) + jnp.where(g < G - 1, 1, 0))
+    greets = [jnp.where(near, 1, 0) for near in (g > 0, g < G - 1, r > 0)]
+    pl.semaphore_wait(barrier, sum(greets))
     rows_all = band + 2 * EDGE
     ahead = lax.rem(g + 1, G)
 
@@ -99,8 +103,18 @@
     def head_copy():
         return span_copy(0, 0, BLOCK + SIDE)
 
+    grouped = (blocks - 4) // GROUP * GROUP
+
+    def group_copy(n):
+        k = n * GROUP + 1
+        return span_copy(k, pl.multiple_of(k * BLOCK + SIDE, SIDE), GROUP * BLOCK)
+
     def middle_copy(k):
         return span_copy(k, pl.multiple_of(k * BLOCK + SIDE, SIDE), BLOCK)
+
+    def each_middle(act):
+        lax.fori_loop(0, grouped // GROUP, lambda n, z: (act(group_copy(n)), z)[1], 0)
+        lax.fori_loop(grouped + 1, blocks - 1, lambda k, z: (act(middle_copy(k)), z)[1], 0)
 
     def tail_copy():
         return span_copy(blocks - 1, width - BLOCK + SIDE, BLOCK - SIDE)
@@ -131,7 +145,7 @@
     @pl.when(g < G - 1)
     def _():
         head_copy().start()
-        lax.fori_loop(1, blocks - 1, lambda k, z: (middle_copy(k).start(), z)[1], 0)
+        each_middle(lambda copy: copy.start())
         tail_copy().start()
 
     prev[:, 0:SIDE] = jnp.zeros((rows_all, SIDE), bf16)
@@ -179,13 +193,26 @@
             own_peaks = jnp.where(lane == 6 * patches + p, peaks[0, 1, i, j].astype(f32), own_peaks)
     extra[...] = jnp.where(r == 0, own_peaks, jnp.zeros((1, 128), f32))
 
+    @pl.when(r < R - 1)
+    def _():
+        pl.semaphore_wait(ready.at[1], 1)
+
+    @pl.when(r > 0)
+    def _():
+        pl.semaphore_signal(ready.at[1], inc=1, device_id={"rows": r - 1}, device_id_type=MESH)
+        pl.semaphore_wait(ready.at[2], 1)
+
+    @pl.when(r < R - 1)
+    def _():
+        pl.semaphore_signal(ready.at[2], inc=1, device_id={"rows": r + 1}, device_id_type=MESH)
+
     @pl.when(g < G - 1)
     def _():
-        pl.semaphore_wait(ready, 1)
+        pl.semaphore_wait(ready.at[0], 1)
 
     @pl.when(g > 0)
     def _():
-        pl.semaphore_signal(ready, inc=1, device_id={"gz": g - 1}, device_id_type=MESH)
+        pl.semaphore_signal(ready.at[0], inc=1, device_id={"gz": g - 1}, device_id_type=MESH)
         edge_copy(0).wait_recv()
 
         @pl.when(r > 0)
@@ -212,7 +239,11 @@
         return sum(value[:, q : q + 128] for q in range(0, BLOCK, 128))
 
     def body(c, z):
-        @pl.when((g > 0) & (c > 0) & (c < blocks - 1))
+        @pl.when((g > 0) & (c % GROUP == 1) & (c <= grouped))
+        def _():
+            group_copy(c // GROUP).wait_recv()
+
+        @pl.when((g > 0) & (c > grouped) & (c < blocks - 1))
         def _():
             middle_copy(c).wait_recv()
 
@@ -267,7 +298,7 @@
             device_id={"rows": lax.rem(r + 1, R)}, device_id_type=MESH)
 
     def send_sums(i, z):
-        d = G - 1 - g - i
+        d = i
         for k in range(R):
             if k:
                 sum_copy(d, k).start()
@@ -284,7 +315,7 @@
         edge_copy(0).wait_send()
         edge_copy(1).wait_send()
         head_copy().wait_send()
-        lax.fori_loop(1, blocks - 1, lambda k, z: (middle_copy(k).wait_send(), z)[1], 0)
+        each_middle(lambda copy: copy.wait_send())
         tail_copy().wait_send()
 
     @pl.when((g > 0) & (r > 0))
@@ -432,11 +463,11 @@
             pltpu.VMEM((R, G, 128), f32),
             pltpu.VMEM((1, 128), f32),
             pltpu.SMEM((1, 2, pgy, pgx), jnp.int32),
-            dma, dma((3,)), pltpu.SemaphoreType.REGULAR, dma((blocks + 2,)), dma((blocks + 2,)), dma((2,)), dma((2,)),
+            dma, dma((3,)), pltpu.SemaphoreType.REGULAR((3,)), dma((blocks + 2,)), dma((blocks + 2,)), dma((2,)), dma((2,)),
             dma((G * R,)), dma((G * R,)),
         ],
         compiler_params=pltpu.CompilerParams(collective_id=0, has_side_effects=True, vmem_limit_bytes=20 * 2**20),
-    )(peaks, sections)
+    )(pltpu.with_memory_space_constraint(peaks, pltpu.HBM), pltpu.with_memory_space_constraint(sections, pltpu.HBM))
     start = (lax.axis_index("rows") * band).astype(jnp.int32).reshape(1)
     field, offsets, residual = pl.pallas_call(
         functools.partial(spread_out, pgy, pgx),

time: 61.4 us -> 59 us (0.961)
  local copies, waits for them, and re-layouts: 2.26 us -> 0 us
    unnamed x4 -> x0, local copies, waits for them, and re-layouts: 2.26 us -> none
where the time goes in v2:
time: 59 us; the launch traced here: 58.9 us
  Pallas kernels  58.2 us (99%)
  between operations  0.64 us (1%)
    pallas_call x1, Pallas kernels, per_device(): pl.pallas_call(functools.partial(register, G, R, pgy, pgx, table), name='...  53.6 us
    pallas_call x1, Pallas kernels, per_device(): pl.pallas_call(functools.partial(spread_out, pgy, pgx), name='spread_out'...  4.62 us

profile of v2, /device:TPU:8, one launch (start us, length us, event | category | flops | bytes accessed | tf_op | source)
XLA Modules:
  0.0 58.9 jit_solution(18083113816402417725)
XLA Ops:
  0.6 53.6 %register.1 = (bf16[1,256,4096]{2,1,0:T(8,128)(2,1)S(1)}, f32[8,128]{1,0:T(8,128)S(1)}) custom-call(s32[1,2,1,4]{3,2,1,0:T(1,128)} %peaks_hbm.1, bf16[1,256,4096]{2,1,0:T(8,128)(2,1)} %sec.1), custom_call_target="tpu_custom_call" | custom-call | tf_op jit(solution)/shard_map/register/pallas_call | solution.py:450
  54.3 4.6 %spread_out.1 = (f32[1,2,256,4096]{3,2,1,0:T(8,128)}, f32[2,4]{1,0:T(2,128)}, bf16[1,256,4096]{2,1,0:T(8,128)(2,1)}) custom-call(s32[1]{0:T(128)} %bitcast.start_ref, f32[8,128]{1,0:T(8,128)S(1)} %get-tuple-element.8.nodes, bf16[1,256,4096]{2,1,0:T(8,128)(2,1)S(1)} %get-tuple-element.9.res_in), custom_call_target="tpu_custom_call" | custom-call | tf_op jit(solution)/shard_map/spread_out/pallas_call | solution.py:472

commit v3 on v2

--- a/solution.py
+++ b/solution.py
@@ -15,7 +15,6 @@
 EDGE = 32
 SIDE = 128
 BLOCK = 256
-TILE = 64
 GROUP = 4
 MESH = pl.DeviceIdType.MESH
 
@@ -43,7 +42,7 @@
     return invert_three(gram) @ design.T
 
 
-def register(G, R, pgy, pgx, table, peaks_hbm, sec, res, nodes, prev, cur, rmat, cmat, gmat, acc,
+def register(G, R, pgy, pgx, table, peaks_hbm, sec, res, nodes, prev, cur, cmat, gmat, shifted, sloped, acc,
              gather, extra, peaks, peak_sem, cur_sem, ready, send_sem, recv_sem, rel_send, rel_recv,
              sum_send, sum_recv):
     band, width = sec.shape[1], sec.shape[2]
@@ -90,34 +89,31 @@
         return pltpu.make_async_remote_copy(
             src_ref=cur.at[pl.ds(row, EDGE), :],
             dst_ref=prev.at[pl.ds(EDGE + row, EDGE), pl.ds(SIDE, width)],
-            send_sem=send_sem.at[which], recv_sem=recv_sem.at[which],
+            send_sem=send_sem, recv_sem=recv_sem.at[which],
             device_id={"gz": ahead}, device_id_type=MESH)
 
-    def span_copy(k, col, count):
+    def span_copy(index, col, count):
         return pltpu.make_async_remote_copy(
             src_ref=cur.at[pl.ds(EDGE, band - 2 * EDGE), pl.ds(col, count)],
             dst_ref=prev.at[pl.ds(2 * EDGE, band - 2 * EDGE), pl.ds(SIDE + col, count)],
-            send_sem=send_sem.at[2 + k], recv_sem=recv_sem.at[2 + k],
+            send_sem=send_sem, recv_sem=recv_sem.at[2 + index],
             device_id={"gz": ahead}, device_id_type=MESH)
 
     def head_copy():
         return span_copy(0, 0, BLOCK + SIDE)
 
     grouped = (blocks - 4) // GROUP * GROUP
+    singles = grouped // GROUP - grouped
 
     def group_copy(n):
         k = n * GROUP + 1
-        return span_copy(k, pl.multiple_of(k * BLOCK + SIDE, SIDE), GROUP * BLOCK)
+        return span_copy(1 + n, pl.multiple_of(k * BLOCK + SIDE, SIDE), GROUP * BLOCK)
 
     def middle_copy(k):
-        return span_copy(k, pl.multiple_of(k * BLOCK + SIDE, SIDE), BLOCK)
-
-    def each_middle(act):
-        lax.fori_loop(0, grouped // GROUP, lambda n, z: (act(group_copy(n)), z)[1], 0)
-        lax.fori_loop(grouped + 1, blocks - 1, lambda k, z: (act(middle_copy(k)), z)[1], 0)
+        return span_copy(singles + k, pl.multiple_of(k * BLOCK + SIDE, SIDE), BLOCK)
 
     def tail_copy():
-        return span_copy(blocks - 1, width - BLOCK + SIDE, BLOCK - SIDE)
+        return span_copy(singles + blocks - 1, width - BLOCK + SIDE, BLOCK - SIDE)
 
     def relay_up():
         return pltpu.make_async_remote_copy(
@@ -145,7 +141,8 @@
     @pl.when(g < G - 1)
     def _():
         head_copy().start()
-        each_middle(lambda copy: copy.start())
+        lax.fori_loop(0, grouped // GROUP, lambda n, z: (group_copy(n).start(), z)[1], 0)
+        lax.fori_loop(grouped + 1, blocks - 1, lambda k, z: (middle_copy(k).start(), z)[1], 0)
         tail_copy().start()
 
     prev[:, 0:SIDE] = jnp.zeros((rows_all, SIDE), bf16)
@@ -169,19 +166,17 @@
 
     patch_row = r * band // PATCH
     peak_load.wait()
-    rr = lax.broadcasted_iota(jnp.int32, (TILE, TILE + 2 * EDGE), 0)
-    rk = lax.broadcasted_iota(jnp.int32, (TILE, TILE + 2 * EDGE), 1)
     ck = lax.broadcasted_iota(jnp.int32, (BLOCK + 2 * SIDE, BLOCK), 0)
     cn = lax.broadcasted_iota(jnp.int32, (BLOCK + 2 * SIDE, BLOCK), 1)
-    rdiff = rk - rr - EDGE
     cdiff = ck - cn - SIDE
-    for j in range(pgx):
-        a = peaks[0, 0, patch_row, j]
+
+    def build(j, z):
         b = peaks[0, 1, patch_row, j]
-        for n, step in enumerate((0, 1, -1)):
-            rmat[j, n * TILE : (n + 1) * TILE, :] = jnp.where(rdiff == a + step, 1.0, 0.0).astype(bf16)
         cmat[j] = jnp.where(cdiff == b, 1.0, 0.0).astype(bf16)
         gmat[j] = jnp.where(cdiff == b + 1, 0.5, jnp.where(cdiff == b - 1, -0.5, 0.0)).astype(bf16)
+        return z
+
+    lax.fori_loop(0, pgx, build, 0)
     acc[...] = jnp.zeros_like(acc)
 
     lane = lax.broadcasted_iota(jnp.int32, (1, 128), 1)
@@ -232,12 +227,6 @@
 
         head_copy().wait_recv()
 
-    tiles = band // TILE
-
-    def fold(value):
-        value = jnp.sum(value.reshape(value.shape[0] // 8, 8, BLOCK), axis=0)
-        return sum(value[:, q : q + 128] for q in range(0, BLOCK, 128))
-
     def body(c, z):
         @pl.when((g > 0) & (c % GROUP == 1) & (c <= grouped))
         def _():
@@ -253,21 +242,25 @@
 
         j = c // per_patch
         col = pl.multiple_of(c * BLOCK, BLOCK)
-        moved = []
-        for t in range(tiles):
-            window = prev[t * TILE : t * TILE + TILE + 2 * EDGE, pl.ds(col, BLOCK + 2 * SIDE)]
-            moved.append(jnp.dot(rmat[j], window, preferred_element_type=f32).astype(bf16))
-        parts = [jnp.concatenate([m[n * TILE : (n + 1) * TILE] for m in moved], axis=0) for n in range(3)]
-        q = jnp.dot(parts[0], cmat[j], preferred_element_type=f32)
-        lower = jnp.dot(parts[1], cmat[j], preferred_element_type=f32)
-        upper = jnp.dot(parts[2], cmat[j], preferred_element_type=f32)
-        gx = jnp.dot(parts[0], gmat[j], preferred_element_type=f32)
-        gy = (lower - upper) * 0.5
-        e = cur[:, pl.ds(col, BLOCK)].astype(f32) - q
-        res[0, :, pl.ds(col, BLOCK)] = e.astype(bf16)
-        for m, value in enumerate((gy * gy, gy * gx, gx * gx, gy * e, gx * e)):
+        window = prev[:, pl.ds(col, BLOCK + 2 * SIDE)]
+        moved = jnp.dot(window, cmat[j], preferred_element_type=f32)
+        slope = jnp.dot(window, gmat[j], preferred_element_type=f32)
+        down = EDGE + peaks[0, 0, patch_row, j]
+        sums = [jnp.zeros((8, 128), f32) for _ in range(5)]
+        for n in range(BLOCK // 128):
+            shifted[n] = moved[:, n * 128 : (n + 1) * 128]
+            sloped[n] = slope[:, n * 128 : (n + 1) * 128]
+        for n in range(BLOCK // 128):
+            q = shifted[n, pl.ds(down, band), :]
+            gy = (shifted[n, pl.ds(down + 1, band), :] - shifted[n, pl.ds(down - 1, band), :]) * 0.5
+            gx = sloped[n, pl.ds(down, band), :]
+            e = cur[:, pl.ds(col + n * 128, 128)].astype(f32) - q
+            res[0, :, pl.ds(col + n * 128, 128)] = e.astype(bf16)
+            for m, value in enumerate((gy * gy, gy * gx, gx * gx, gy * e, gx * e)):
+                sums[m] = sums[m] + jnp.sum(value.reshape(band // 8, 8, 128), axis=0)
+        for m, value in enumerate(sums):
             at = pl.ds(pl.multiple_of((m * pgx + j) * 8, 8), 8)
-            acc[at, :] = acc[at, :] + fold(value)
+            acc[at, :] = acc[at, :] + value
         return z
 
     lax.fori_loop(0, blocks, body, 0)
@@ -282,20 +275,18 @@
         place = place + jnp.where(lax.broadcasted_iota(jnp.int32, (count, 128), 0) >= m * pgx, patches - pgx, 0)
     hit = lax.broadcasted_iota(jnp.int32, (count, 128), 1) == place + patch_row * pgx
     mine = jnp.sum(jnp.where(hit, totals, 0.0), axis=0, keepdims=True)
-    gather[r, pl.ds(g, 1), :] = mine + extra[...]
+    slot = pl.ds(r * G + g, 1)
+    gather[slot, :] = mine + extra[...]
 
     def sum_copy(d, k):
         return pltpu.make_async_remote_copy(
-            src_ref=gather.at[r, pl.ds(g, 1), :], dst_ref=gather.at[r, pl.ds(g, 1), :],
-            send_sem=sum_send.at[d * R + k], recv_sem=sum_recv.at[r * G + g],
+            src_ref=gather.at[slot], dst_ref=gather.at[slot], send_sem=sum_send, recv_sem=sum_recv,
             device_id={"gz": g + d, "rows": lax.rem(r + k, R)}, device_id_type=MESH)
 
-    def sum_arrival(s, k):
-        origin = lax.rem(r + k, R)
-        return pltpu.make_async_remote_copy(
-            src_ref=gather.at[origin, pl.ds(s, 1), :], dst_ref=gather.at[origin, pl.ds(s, 1), :],
-            send_sem=sum_send.at[0], recv_sem=sum_recv.at[origin * G + s],
-            device_id={"rows": lax.rem(r + 1, R)}, device_id_type=MESH)
+    def all_sums(count):
+        return pltpu.make_async_remote_copy(
+            src_ref=gather.at[pl.ds(0, count)], dst_ref=gather.at[pl.ds(0, count)],
+            send_sem=sum_send, recv_sem=sum_recv, device_id={"rows": lax.rem(r + 1, R)}, device_id_type=MESH)
 
     def send_sums(i, z):
         d = i
@@ -312,11 +303,9 @@
 
     @pl.when(g < G - 1)
     def _():
-        edge_copy(0).wait_send()
-        edge_copy(1).wait_send()
-        head_copy().wait_send()
-        each_middle(lambda copy: copy.wait_send())
-        tail_copy().wait_send()
+        pltpu.make_async_remote_copy(
+            src_ref=cur, dst_ref=cur, send_sem=send_sem, recv_sem=recv_sem.at[0],
+            device_id={"gz": ahead}, device_id_type=MESH).wait_send()
 
     @pl.when((g > 0) & (r > 0))
     def _():
@@ -326,33 +315,15 @@
     def _():
         relay_down().wait_send()
 
-    def settle_sums(d, z):
-        for k in range(R):
-            if k:
-                sum_copy(d, k).wait_send()
-            else:
-                @pl.when(d > 0)
-                def _():
-                    sum_copy(d, k).wait_send()
-        return z
-
-    lax.fori_loop(0, G - g, settle_sums, 0)
-
-    def await_sums(s, z):
-        for k in range(R):
-            if k:
-                sum_arrival(s, k).wait_recv()
-            else:
-                @pl.when(s < g)
-                def _():
-                    sum_arrival(s, k).wait_recv()
-        return z
-
-    lax.fori_loop(0, g + 1, await_sums, 0)
-
-    full = gather[0]
+    for s in range(G):
+        @pl.when(g == s)
+        def _():
+            all_sums(R * (G - s) - 1).wait_send()
+            all_sums(R * (s + 1) - 1).wait_recv()
+
+    full = gather[0:G]
     for k in range(1, R):
-        full = full + gather[k]
+        full = full + gather[k * G : (k + 1) * G]
 
     def moment(m):
         return pltpu.roll(full, 128 - m * patches, 1)
@@ -396,7 +367,7 @@
     nodes[4:8] = jnp.zeros((4, 128), f32)
 
 
-def spread_out(pgy, pgx, start_ref, nodes, res_in, field, offsets, res_out, buf, out_sem, field_sem):
+def spread_out(pgy, pgx, nodes, res_in, field, offsets, res_out, buf, out_sem, field_sem):
     band, width = field.shape[2], field.shape[3]
     f32 = jnp.float32
     put = pltpu.make_async_copy(res_in, res_out, out_sem)
@@ -405,7 +376,6 @@
     cols = jnp.clip(cols, 0.0, pgx - 1.0)
     weights = [jnp.maximum(0.0, 1.0 - jnp.abs(cols - j)) for j in range(pgx)]
     part = 32
-    copies = []
     for k in range(2):
         wide = []
         for i in range(pgy):
@@ -420,19 +390,15 @@
                 if pgy == 1:
                     block = wide[0]
                 else:
-                    rows = lax.broadcasted_iota(jnp.int32, (8, 1), 0).astype(f32) + start_ref[0].astype(f32)
+                    rows = (lax.broadcasted_iota(jnp.int32, (8, 1), 0) + lax.axis_index("rows") * band).astype(f32)
                     pos = jnp.clip((rows + (t * part + q + 0.5)) / PATCH - 0.5, 0.0, pgy - 1.0)
                     block = sum(jnp.maximum(0.0, 1.0 - jnp.abs(pos - i)) * wide[i] for i in range(pgy))
                 buf[k, slot * part + q : slot * part + q + 8, :] = block
-            copy = pltpu.make_async_copy(
-                buf.at[k, pl.ds(slot * part, part), :], field.at[0, k, pl.ds(t * part, part), :],
-                field_sem.at[len(copies)])
-            copy.start()
-            copies.append(copy)
+            pltpu.make_async_copy(
+                buf.at[k, pl.ds(slot * part, part), :], field.at[0, k, pl.ds(t * part, part), :], field_sem).start()
     offsets[...] = nodes[2:4, 0 : pgy * pgx]
     put.wait()
-    for copy in copies:
-        copy.wait()
+    pltpu.make_async_copy(field, field, field_sem).wait()
 
 
 def per_device(G, R, sections, peaks):
@@ -443,10 +409,11 @@
     f32, bf16 = jnp.float32, jnp.bfloat16
     table = fit_table(pgy, pgx, PATCH, height, width).astype(np.float32)
     vmem = pl.BlockSpec(memory_space=pltpu.VMEM)
-    smem = pl.BlockSpec(memory_space=pltpu.SMEM)
     anywhere = pl.BlockSpec(memory_space=pl.ANY)
     dma = pltpu.SemaphoreType.DMA
     padded = -(-5 * pgx // 8) * 8
+    grouped = (blocks - 4) // GROUP * GROUP
+    arrivals = 2 + blocks - grouped + grouped // GROUP
     residual, nodes = pl.pallas_call(
         functools.partial(register, G, R, pgy, pgx, table),
         name="register",
@@ -456,19 +423,19 @@
         scratch_shapes=[
             pltpu.VMEM((band + 2 * EDGE, width + 2 * SIDE), bf16),
             pltpu.VMEM((band, width), bf16),
-            pltpu.VMEM((pgx, 3 * TILE, TILE + 2 * EDGE), bf16),
             pltpu.VMEM((pgx, BLOCK + 2 * SIDE, BLOCK), bf16),
             pltpu.VMEM((pgx, BLOCK + 2 * SIDE, BLOCK), bf16),
+            pltpu.VMEM((BLOCK // 128, band + 2 * EDGE, 128), f32),
+            pltpu.VMEM((BLOCK // 128, band + 2 * EDGE, 128), f32),
             pltpu.VMEM((8 * padded, 128), f32),
-            pltpu.VMEM((R, G, 128), f32),
+            pltpu.VMEM((R * G, 128), f32),
             pltpu.VMEM((1, 128), f32),
             pltpu.SMEM((1, 2, pgy, pgx), jnp.int32),
-            dma, dma((3,)), pltpu.SemaphoreType.REGULAR((3,)), dma((blocks + 2,)), dma((blocks + 2,)), dma((2,)), dma((2,)),
-            dma((G * R,)), dma((G * R,)),
+            dma, dma((3,)), pltpu.SemaphoreType.REGULAR((3,)), dma, dma((arrivals,)), dma((2,)), dma((2,)),
+            dma, dma,
         ],
         compiler_params=pltpu.CompilerParams(collective_id=0, has_side_effects=True, vmem_limit_bytes=20 * 2**20),
     )(pltpu.with_memory_space_constraint(peaks, pltpu.HBM), pltpu.with_memory_space_constraint(sections, pltpu.HBM))
-    start = (lax.axis_index("rows") * band).astype(jnp.int32).reshape(1)
     field, offsets, residual = pl.pallas_call(
         functools.partial(spread_out, pgy, pgx),
         name="spread_out",
@@ -477,11 +444,11 @@
             jax.ShapeDtypeStruct((2, pgy * pgx), f32),
             jax.ShapeDtypeStruct((1, band, width), bf16),
         ),
-        in_specs=[smem, vmem, vmem],
+        in_specs=[vmem, vmem],
         out_specs=(anywhere, vmem, anywhere),
-        scratch_shapes=[pltpu.VMEM((2, 32 if pgy == 1 else band, width), f32), dma, dma((2 * (band // 32),))],
+        scratch_shapes=[pltpu.VMEM((2, 32 if pgy == 1 else band, width), f32), dma, dma],
         compiler_params=pltpu.CompilerParams(vmem_limit_bytes=20 * 2**20),
-    )(start, nodes, residual)
+    )(nodes, residual)
     return field, offsets.reshape(1, 2, pgy, pgx), residual
 
 

time: 59 us -> 57.7 us (0.978)
  Pallas kernels: 58.2 us -> 56.9 us
    pallas_call x1, Pallas kernels: 53.6 us -> 52.4 us  [per_device(): pl.pallas_call(functools.partial(register, G, R, pgy, pgx, table), name='...]
where the time goes in v3:
time: 57.7 us; the launch traced here: 57.6 us
  Pallas kernels  56.9 us (99%)
  between operations  0.64 us (1%)
    pallas_call x1, Pallas kernels, per_device(): pl.pallas_call(functools.partial(register, G, R, pgy, pgx, table), name='...  52.4 us
    pallas_call x1, Pallas kernels, per_device(): pl.pallas_call(functools.partial(spread_out, pgy, pgx), name='spread_out'...  4.48 us

profile of v3, /device:TPU:8, one launch (start us, length us, event | category | flops | bytes accessed | tf_op | source)
XLA Modules:
  0.0 57.6 jit_solution(10539079394426885309)
XLA Ops:
  0.6 52.4 %register.1 = (bf16[1,256,4096]{2,1,0:T(8,128)(2,1)S(1)}, f32[8,128]{1,0:T(8,128)S(1)}) custom-call(s32[1,2,1,4]{3,2,1,0:T(1,128)} %peaks_hbm.1, bf16[1,256,4096]{2,1,0:T(8,128)(2,1)} %sec.1), custom_call_target="tpu_custom_call" | custom-call | tf_op jit(solution)/shard_map/register/pallas_call | solution.py:417
  53.1 4.5 %spread_out.1 = (f32[1,2,256,4096]{3,2,1,0:T(8,128)}, f32[2,4]{1,0:T(2,128)}, bf16[1,256,4096]{2,1,0:T(8,128)(2,1)}) custom-call(f32[8,128]{1,0:T(8,128)S(1)} %get-tuple-element.8.nodes, bf16[1,256,4096]{2,1,0:T(8,128)(2,1)S(1)} %get-tuple-element.9.res_in), custom_call_target="tpu_custom_call" | custom-call | tf_op jit(solution)/shard_map/spread_out/pallas_call | solution.py:439

commit v4 on v3

--- a/solution.py
+++ b/solution.py
@@ -16,6 +16,7 @@
 SIDE = 128
 BLOCK = 256
 GROUP = 4
+LATE = 2
 MESH = pl.DeviceIdType.MESH
 
 
@@ -44,7 +45,7 @@
 
 def register(G, R, pgy, pgx, table, peaks_hbm, sec, res, nodes, prev, cur, cmat, gmat, shifted, sloped, acc,
              gather, extra, peaks, peak_sem, cur_sem, ready, send_sem, recv_sem, rel_send, rel_recv,
-             sum_send, sum_recv):
+             sum_send, sum_recv, late, shift_row, shifts, late_send, late_recv, shift_recv, rows_send, rows_recv, late_acc):
     band, width = sec.shape[1], sec.shape[2]
     height = band * R
     blocks = width // BLOCK
@@ -82,6 +83,7 @@
     greets = [jnp.where(near, 1, 0) for near in (g > 0, g < G - 1, r > 0)]
     pl.semaphore_wait(barrier, sum(greets))
     rows_all = band + 2 * EDGE
+    reach = LATE * BLOCK + SIDE
     ahead = lax.rem(g + 1, G)
 
     def edge_copy(which):
@@ -119,14 +121,20 @@
         return pltpu.make_async_remote_copy(
             src_ref=prev.at[pl.ds(EDGE, EDGE), pl.ds(SIDE, width)],
             dst_ref=prev.at[pl.ds(EDGE + band, EDGE), pl.ds(SIDE, width)],
-            send_sem=rel_send.at[0], recv_sem=rel_recv.at[0],
+            send_sem=rel_send, recv_sem=rel_recv,
             device_id={"rows": lax.rem(r + R - 1, R)}, device_id_type=MESH)
 
     def relay_down():
         return pltpu.make_async_remote_copy(
             src_ref=prev.at[pl.ds(band, EDGE), pl.ds(SIDE, width)],
             dst_ref=prev.at[pl.ds(0, EDGE), pl.ds(SIDE, width)],
-            send_sem=rel_send.at[1], recv_sem=rel_recv.at[1],
+            send_sem=rel_send, recv_sem=rel_recv,
+            device_id={"rows": lax.rem(r + 1, R)}, device_id_type=MESH)
+
+    def both_relays(count):
+        rows = pl.ds(0, count * EDGE)
+        return pltpu.make_async_remote_copy(
+            src_ref=cur.at[rows, :], dst_ref=cur.at[rows, :], send_sem=rel_send, recv_sem=rel_recv,
             device_id={"rows": lax.rem(r + 1, R)}, device_id_type=MESH)
 
     for which in (0, 1):
@@ -201,51 +209,124 @@
     def _():
         pl.semaphore_signal(ready.at[2], inc=1, device_id={"rows": r + 1}, device_id_type=MESH)
 
+    @pl.when(g > 0)
+    def _():
+        pl.semaphore_wait(ready.at[3], 1)
+
     @pl.when(g < G - 1)
     def _():
+        pl.semaphore_signal(ready.at[3], inc=1, device_id={"gz": g + 1}, device_id_type=MESH)
+
+    region = pl.ds(width - reach, reach)
+    late[:, :, reach:] = jnp.zeros((G, rows_all, SIDE), bf16)
+
+    @pl.when(r == 0)
+    def _():
+        late[:, 0:EDGE, :] = jnp.zeros((G, EDGE, reach + SIDE), bf16)
+
+    @pl.when(r == R - 1)
+    def _():
+        late[:, EDGE + band :, :] = jnp.zeros((G, EDGE, reach + SIDE), bf16)
+
+    def late_body():
+        return pltpu.make_async_remote_copy(
+            src_ref=cur.at[:, region], dst_ref=late.at[g, pl.ds(EDGE, band), pl.ds(0, reach)],
+            send_sem=late_send.at[0], recv_sem=late_recv.at[g],
+            device_id={"gz": 0}, device_id_type=MESH)
+
+    def late_section(s, rows):
+        ref = late.at[s, pl.ds(0, rows), pl.ds(0, reach)]
+        return pltpu.make_async_remote_copy(
+            src_ref=ref, dst_ref=ref, send_sem=late_send.at[0], recv_sem=late_recv.at[s],
+            device_id={"rows": lax.rem(r + 1, R)}, device_id_type=MESH)
+
+    def await_section(s, rows):
+        @pl.when((r == 0) | (r == R - 1))
+        def _():
+            late_section(s, rows + EDGE).wait_recv()
+
+        @pl.when((r > 0) & (r < R - 1))
+        def _():
+            late_section(s, rows + 2 * EDGE).wait_recv()
+
+    def late_edge(up):
+        source = pl.ds(0 if up else band - EDGE, EDGE)
+        target = pl.ds(EDGE + band if up else 0, EDGE)
+        return pltpu.make_async_remote_copy(
+            src_ref=cur.at[source, region], dst_ref=late.at[g, target, pl.ds(0, reach)],
+            send_sem=late_send.at[1], recv_sem=late_recv.at[g],
+            device_id={"gz": 0, "rows": lax.rem(r + (R - 1 if up else 1), R)}, device_id_type=MESH)
+
+    def late_edges(count):
+        ref = late.at[0, pl.ds(0, count * EDGE), pl.ds(0, reach)]
+        return pltpu.make_async_remote_copy(
+            src_ref=ref, dst_ref=ref, send_sem=late_send.at[1], recv_sem=late_recv.at[0],
+            device_id={"rows": lax.rem(r + 1, R)}, device_id_type=MESH)
+
+    def late_peak():
+        return pltpu.make_async_remote_copy(
+            src_ref=shift_row, dst_ref=shifts.at[pl.ds(g, 1)], send_sem=late_send.at[2], recv_sem=shift_recv,
+            device_id={"gz": 0}, device_id_type=MESH)
+
+    def late_peaks():
+        ref = shifts.at[pl.ds(1, G - 1)]
+        return pltpu.make_async_remote_copy(
+            src_ref=ref, dst_ref=ref, send_sem=late_send.at[2], recv_sem=shift_recv,
+            device_id={"rows": lax.rem(r + 1, R)}, device_id_type=MESH)
+
+    shift_row[...] = jnp.where(lane == 0, peaks[0, 0, patch_row, pgx - 1], peaks[0, 1, patch_row, pgx - 1])
+
+    @pl.when(g == 0)
+    def _():
+        late[0, EDGE : EDGE + band, 0:reach] = cur[:, width - reach :]
+
+    @pl.when(g > 0)
+    def _():
+        late_body().start()
+        late_peak().start()
+
+    @pl.when(r > 0)
+    def _():
+        late_edge(True).start()
+
+    @pl.when(r < R - 1)
+    def _():
+        late_edge(False).start()
+
+    @pl.when(g > 0)
+    def _():
+        edge_copy(0).wait_recv()
+
+        @pl.when(r > 0)
+        def _():
+            relay_up().start()
+
+        edge_copy(1).wait_recv()
+
+        @pl.when(r < R - 1)
+        def _():
+            relay_down().start()
+
+        @pl.when((r == 0) | (r == R - 1))
+        def _():
+            both_relays(1).wait_recv()
+
+        @pl.when((r > 0) & (r < R - 1))
+        def _():
+            both_relays(2).wait_recv()
+
+    @pl.when((g > 0) & (g < G - 1))
+    def _():
         pl.semaphore_wait(ready.at[0], 1)
 
     @pl.when(g > 0)
     def _():
         pl.semaphore_signal(ready.at[0], inc=1, device_id={"gz": g - 1}, device_id_type=MESH)
-        edge_copy(0).wait_recv()
-
-        @pl.when(r > 0)
-        def _():
-            relay_up().start()
-
-        edge_copy(1).wait_recv()
-
-        @pl.when(r < R - 1)
-        def _():
-            relay_down().start()
-            relay_up().wait_recv()
-
-        @pl.when(r > 0)
-        def _():
-            relay_down().wait_recv()
-
         head_copy().wait_recv()
 
-    def body(c, z):
-        @pl.when((g > 0) & (c % GROUP == 1) & (c <= grouped))
-        def _():
-            group_copy(c // GROUP).wait_recv()
-
-        @pl.when((g > 0) & (c > grouped) & (c < blocks - 1))
-        def _():
-            middle_copy(c).wait_recv()
-
-        @pl.when((g > 0) & (c == blocks - 1))
-        def _():
-            tail_copy().wait_recv()
-
-        j = c // per_patch
-        col = pl.multiple_of(c * BLOCK, BLOCK)
-        window = prev[:, pl.ds(col, BLOCK + 2 * SIDE)]
-        moved = jnp.dot(window, cmat[j], preferred_element_type=f32)
-        slope = jnp.dot(window, gmat[j], preferred_element_type=f32)
-        down = EDGE + peaks[0, 0, patch_row, j]
+    def correlate(window, columns, gradients, down, current, keep):
+        moved = jnp.dot(window, columns, preferred_element_type=f32)
+        slope = jnp.dot(window, gradients, preferred_element_type=f32)
         sums = [jnp.zeros((8, 128), f32) for _ in range(5)]
         for n in range(BLOCK // 128):
             shifted[n] = moved[:, n * 128 : (n + 1) * 128]
@@ -254,18 +335,48 @@
             q = shifted[n, pl.ds(down, band), :]
             gy = (shifted[n, pl.ds(down + 1, band), :] - shifted[n, pl.ds(down - 1, band), :]) * 0.5
             gx = sloped[n, pl.ds(down, band), :]
-            e = cur[:, pl.ds(col + n * 128, 128)].astype(f32) - q
-            res[0, :, pl.ds(col + n * 128, 128)] = e.astype(bf16)
+            e = current(n).astype(f32) - q
+            keep(n, e)
             for m, value in enumerate((gy * gy, gy * gx, gx * gx, gy * e, gx * e)):
                 sums[m] = sums[m] + jnp.sum(value.reshape(band // 8, 8, 128), axis=0)
+        return sums
+
+    def body(c, z):
+        @pl.when((g > 0) & (c % GROUP == 1) & (c <= grouped))
+        def _():
+            group_copy(c // GROUP).wait_recv()
+
+        @pl.when((g > 0) & (c > grouped) & (c < blocks - 1))
+        def _():
+            middle_copy(c).wait_recv()
+
+        @pl.when((g > 0) & (c == blocks - 1))
+        def _():
+            tail_copy().wait_recv()
+
+        j = c // per_patch
+        col = pl.multiple_of(c * BLOCK, BLOCK)
+
+        def keep(n, e):
+            res[0, :, pl.ds(col + n * 128, 128)] = e.astype(bf16)
+
+        sums = correlate(prev[:, pl.ds(col, BLOCK + 2 * SIDE)], cmat[j], gmat[j], EDGE + peaks[0, 0, patch_row, j],
+                         lambda n: cur[:, pl.ds(col + n * 128, 128)], keep)
+        spare = acc.shape[0] // 8 - 8
         for m, value in enumerate(sums):
-            at = pl.ds(pl.multiple_of((m * pgx + j) * 8, 8), 8)
+            place = jnp.where(c < blocks - LATE, m * pgx + j, spare + m)
+            at = pl.ds(pl.multiple_of(place * 8, 8), 8)
             acc[at, :] = acc[at, :] + value
         return z
 
-    lax.fori_loop(0, blocks, body, 0)
-
-    count = acc.shape[0] // 8
+    lax.fori_loop(0, blocks - LATE, body, 0)
+
+    @pl.when(g == 0)
+    def _():
+        pl.semaphore_wait(ready.at[0], 1)
+
+
+    count = acc.shape[0] // 8 - 8
     totals = acc[pl.ds(0, count, stride=8), :]
     for k in range(1, 8):
         totals = totals + acc[pl.ds(k, count, stride=8), :]
@@ -301,19 +412,105 @@
 
     lax.fori_loop(0, G - g, send_sums, 0)
 
+    def late_rows(s, k):
+        rows = pl.ds((R + r) * G, G)
+        return pltpu.make_async_remote_copy(
+            src_ref=gather.at[rows], dst_ref=gather.at[rows], send_sem=rows_send.at[s], recv_sem=rows_recv,
+            device_id={"gz": s, "rows": lax.rem(r + k, R)}, device_id_type=MESH)
+
+    def all_rows(s):
+        rows = pl.ds(0, R * G)
+        return pltpu.make_async_remote_copy(
+            src_ref=gather.at[rows], dst_ref=gather.at[rows], send_sem=rows_send.at[s], recv_sem=rows_recv,
+            device_id={"rows": lax.rem(r + 1, R)}, device_id_type=MESH)
+
+    @pl.when(g == 0)
+    def _():
+        late_peaks().wait_recv()
+        await_section(G - 1, band)
+
+        def assist(i, z):
+            s = G - i
+
+            @pl.when(i < G - 1)
+            def _():
+                await_section(s - 1, band)
+
+            @pl.when(i == G - 1)
+            def _():
+                await_section(0, 0)
+
+            a = shifts[s, 0]
+            b = shifts[s, 1]
+            cmat[0] = jnp.where(cdiff == b, 1.0, 0.0).astype(bf16)
+            gmat[0] = jnp.where(cdiff == b + 1, 0.5, jnp.where(cdiff == b - 1, -0.5, 0.0)).astype(bf16)
+            both = [jnp.zeros((8, 128), f32) for _ in range(5)]
+            for k in range(LATE):
+                found = correlate(
+                    late[s - 1, :, k * BLOCK : k * BLOCK + BLOCK + 2 * SIDE], cmat[0], gmat[0], EDGE + a,
+                    lambda n: late[s, EDGE : EDGE + band, SIDE + k * BLOCK + n * 128 : SIDE + k * BLOCK + n * 128 + 128],
+                    lambda n, e: None)
+                both = [old + new for old, new in zip(both, found)]
+            for m, value in enumerate(both):
+                late_acc[pl.ds(pl.multiple_of((m * G + s) * 8, 8), 8), :] = value
+            return z
+
+        late_acc[...] = jnp.zeros_like(late_acc)
+        lax.fori_loop(1, G, assist, 0)
+
+        sums = late_acc[pl.ds(0, 5 * G, stride=8), :]
+        for k in range(1, 8):
+            sums = sums + late_acc[pl.ds(k, 5 * G, stride=8), :]
+        sums = jnp.sum(sums, axis=1, keepdims=True)
+        wide = lax.broadcasted_iota(jnp.int32, (G, 128), 1)
+        lines = jnp.zeros((G, 128), f32)
+        for m in range(5):
+            lines = jnp.where(wide == m * patches + patch_row * pgx + pgx - 1, sums[m * G : (m + 1) * G], lines)
+        gather[pl.ds((R + r) * G, G), :] = lines
+
+        def hand_out(s, z):
+            for k in range(R):
+                late_rows(s, k).start()
+            return z
+
+        lax.fori_loop(1, G, hand_out, 0)
+
+    lax.fori_loop(blocks - LATE, blocks, body, 0)
+
     @pl.when(g < G - 1)
     def _():
         pltpu.make_async_remote_copy(
             src_ref=cur, dst_ref=cur, send_sem=send_sem, recv_sem=recv_sem.at[0],
             device_id={"gz": ahead}, device_id_type=MESH).wait_send()
 
-    @pl.when((g > 0) & (r > 0))
-    def _():
-        relay_up().wait_send()
-
-    @pl.when((g > 0) & (r < R - 1))
-    def _():
-        relay_down().wait_send()
+    @pl.when((g > 0) & ((r == 0) | (r == R - 1)))
+    def _():
+        both_relays(1).wait_send()
+
+    @pl.when((g > 0) & (r > 0) & (r < R - 1))
+    def _():
+        both_relays(2).wait_send()
+
+    @pl.when(g > 0)
+    def _():
+        late_body().wait_send()
+        late_peak().wait_send()
+
+    @pl.when((r == 0) | (r == R - 1))
+    def _():
+        late_edges(1).wait_send()
+
+    @pl.when((r > 0) & (r < R - 1))
+    def _():
+        late_edges(2).wait_send()
+
+    @pl.when(g == 0)
+    def _():
+        lax.fori_loop(1, G, lambda s, z: (all_rows(s).wait_send(), z)[1], 0)
+
+    @pl.when(g > 0)
+    def _():
+        all_rows(0).wait_recv()
 
     for s in range(G):
         @pl.when(g == s)
@@ -322,7 +519,7 @@
             all_sums(R * (s + 1) - 1).wait_recv()
 
     full = gather[0:G]
-    for k in range(1, R):
+    for k in range(1, 2 * R):
         full = full + gather[k * G : (k + 1) * G]
 
     def moment(m):
@@ -427,14 +624,18 @@
             pltpu.VMEM((pgx, BLOCK + 2 * SIDE, BLOCK), bf16),
             pltpu.VMEM((BLOCK // 128, band + 2 * EDGE, 128), f32),
             pltpu.VMEM((BLOCK // 128, band + 2 * EDGE, 128), f32),
-            pltpu.VMEM((8 * padded, 128), f32),
-            pltpu.VMEM((R * G, 128), f32),
+            pltpu.VMEM((8 * (padded + 8), 128), f32),
+            pltpu.VMEM((2 * R * G, 128), f32),
             pltpu.VMEM((1, 128), f32),
             pltpu.SMEM((1, 2, pgy, pgx), jnp.int32),
-            dma, dma((3,)), pltpu.SemaphoreType.REGULAR((3,)), dma, dma((arrivals,)), dma((2,)), dma((2,)),
+            dma, dma((3,)), pltpu.SemaphoreType.REGULAR((4,)), dma, dma((arrivals,)), dma, dma,
             dma, dma,
+            pltpu.VMEM((G, band + 2 * EDGE, LATE * BLOCK + 2 * SIDE), bf16),
+            pltpu.VMEM((1, 128), jnp.int32), pltpu.VMEM((G, 128), jnp.int32),
+            dma((3,)), dma((G,)), dma, dma((G,)), dma,
+            pltpu.VMEM((5 * G * 8, 128), f32),
         ],
-        compiler_params=pltpu.CompilerParams(collective_id=0, has_side_effects=True, vmem_limit_bytes=20 * 2**20),
+        compiler_params=pltpu.CompilerParams(collective_id=0, has_side_effects=True, vmem_limit_bytes=40 * 2**20),
     )(pltpu.with_memory_space_constraint(peaks, pltpu.HBM), pltpu.with_memory_space_constraint(sections, pltpu.HBM))
     field, offsets, residual = pl.pallas_call(
         functools.partial(spread_out, pgy, pgx),

time: 57.7 us -> 57 us (0.988); the launches traced: 57.6 us -> 55.9 us
  Pallas kernels: 56.9 us -> 55.3 us
    pallas_call x1, Pallas kernels: 52.4 us -> 50.8 us  [per_device(): pl.pallas_call(functools.partial(register, G, R, pgy, pgx, table), name='...]
where the time goes in v4:
time: 57 us; the launch traced here: 55.9 us
  Pallas kernels  55.3 us (97%)
  between operations  0.64 us (1%)
    pallas_call x1, Pallas kernels, per_device(): pl.pallas_call(functools.partial(register, G, R, pgy, pgx, table), name='...  50.8 us
    pallas_call x1, Pallas kernels, per_device(): pl.pallas_call(functools.partial(spread_out, pgy, pgx), name='spread_out'...  4.48 us

profile of v4, /device:TPU:8, one launch (start us, length us, event | category | flops | bytes accessed | tf_op | source)
XLA Modules:
  0.0 55.9 jit_solution(17502521852494343171)
XLA Ops:
  0.6 50.8 %register.1 = (bf16[1,256,4096]{2,1,0:T(8,128)(2,1)S(1)}, f32[8,128]{1,0:T(8,128)S(1)}) custom-call(s32[1,2,1,4]{3,2,1,0:T(1,128)} %peaks_hbm.1, bf16[1,256,4096]{2,1,0:T(8,128)(2,1)} %sec.1), custom_call_target="tpu_custom_call" | custom-call | tf_op jit(solution)/shard_map/register/pallas_call | solution.py:614
  51.4 4.5 %spread_out.1 = (f32[1,2,256,4096]{3,2,1,0:T(8,128)}, f32[2,4]{1,0:T(2,128)}, bf16[1,256,4096]{2,1,0:T(8,128)(2,1)}) custom-call(f32[8,128]{1,0:T(8,128)S(1)} %get-tuple-element.8.nodes, bf16[1,256,4096]{2,1,0:T(8,128)(2,1)S(1)} %get-tuple-element.9.res_in), custom_call_target="tpu_custom_call" | custom-call | tf_op jit(solution)/shard_map/spread_out/pallas_call | solution.py:640

commit v5 on v4

--- a/solution.py
+++ b/solution.py
@@ -178,13 +178,6 @@
     cn = lax.broadcasted_iota(jnp.int32, (BLOCK + 2 * SIDE, BLOCK), 1)
     cdiff = ck - cn - SIDE
 
-    def build(j, z):
-        b = peaks[0, 1, patch_row, j]
-        cmat[j] = jnp.where(cdiff == b, 1.0, 0.0).astype(bf16)
-        gmat[j] = jnp.where(cdiff == b + 1, 0.5, jnp.where(cdiff == b - 1, -0.5, 0.0)).astype(bf16)
-        return z
-
-    lax.fori_loop(0, pgx, build, 0)
     acc[...] = jnp.zeros_like(acc)
 
     lane = lax.broadcasted_iota(jnp.int32, (1, 128), 1)
@@ -360,7 +353,10 @@
         def keep(n, e):
             res[0, :, pl.ds(col + n * 128, 128)] = e.astype(bf16)
 
-        sums = correlate(prev[:, pl.ds(col, BLOCK + 2 * SIDE)], cmat[j], gmat[j], EDGE + peaks[0, 0, patch_row, j],
+        b = peaks[0, 1, patch_row, j]
+        cmat[0] = jnp.where(cdiff == b, 1.0, 0.0).astype(bf16)
+        gmat[0] = jnp.where(cdiff == b + 1, 0.5, jnp.where(cdiff == b - 1, -0.5, 0.0)).astype(bf16)
+        sums = correlate(prev[:, pl.ds(col, BLOCK + 2 * SIDE)], cmat[0], gmat[0], EDGE + peaks[0, 0, patch_row, j],
                          lambda n: cur[:, pl.ds(col + n * 128, 128)], keep)
         spare = acc.shape[0] // 8 - 8
         for m, value in enumerate(sums):
@@ -620,8 +616,8 @@
         scratch_shapes=[
             pltpu.VMEM((band + 2 * EDGE, width + 2 * SIDE), bf16),
             pltpu.VMEM((band, width), bf16),
-            pltpu.VMEM((pgx, BLOCK + 2 * SIDE, BLOCK), bf16),
-            pltpu.VMEM((pgx, BLOCK + 2 * SIDE, BLOCK), bf16),
+            pltpu.VMEM((1, BLOCK + 2 * SIDE, BLOCK), bf16),
+            pltpu.VMEM((1, BLOCK + 2 * SIDE, BLOCK), bf16),
             pltpu.VMEM((BLOCK // 128, band + 2 * EDGE, 128), f32),
             pltpu.VMEM((BLOCK // 128, band + 2 * EDGE, 128), f32),
             pltpu.VMEM((8 * (padded + 8), 128), f32),

time: 57 us -> 56.3 us (0.988); the launches traced: 55.9 us -> 56.1 us
  no operation moved by 1% of the time
where the time goes in v5:
time: 56.3 us; the launch traced here: 56.1 us
  Pallas kernels  55.5 us (99%)
  between operations  0.64 us (1%)
    pallas_call x1, Pallas kernels, per_device(): pl.pallas_call(functools.partial(register, G, R, pgy, pgx, table), name='...  51 us
    pallas_call x1, Pallas kernels, per_device(): pl.pallas_call(functools.partial(spread_out, pgy, pgx), name='spread_out'...  4.48 us

profile of v5, /device:TPU:8, one launch (start us, length us, event | category | flops | bytes accessed | tf_op | source)
XLA Modules:
  0.0 56.1 jit_solution(7785819892306102801)
XLA Ops:
  0.6 51.0 %register.1 = (bf16[1,256,4096]{2,1,0:T(8,128)(2,1)S(1)}, f32[8,128]{1,0:T(8,128)S(1)}) custom-call(s32[1,2,1,4]{3,2,1,0:T(1,128)} %peaks_hbm.1, bf16[1,256,4096]{2,1,0:T(8,128)(2,1)} %sec.1), custom_call_target="tpu_custom_call" | custom-call | tf_op jit(solution)/shard_map/register/pallas_call | solution.py:610
  51.6 4.5 %spread_out.1 = (f32[1,2,256,4096]{3,2,1,0:T(8,128)}, f32[2,4]{1,0:T(2,128)}, bf16[1,256,4096]{2,1,0:T(8,128)(2,1)}) custom-call(f32[8,128]{1,0:T(8,128)S(1)} %get-tuple-element.8.nodes, bf16[1,256,4096]{2,1,0:T(8,128)(2,1)S(1)} %get-tuple-element.9.res_in), custom_call_target="tpu_custom_call" | custom-call | tf_op jit(solution)/shard_map/spread_out/pallas_call | solution.py:636
